TPU v7x, 32 devices: a whole 2x2x4 slice. The times are simulated.
32 devices in a mesh: batch: 4 (over x, core), lat: 8 (over z, y).
Axes of the slice: x: 2, y: 2, z: 4, core: 2. Of those that a mesh axis runs over, the one named last changes fastest.
Arguments:
- predicted: bfloat16 [4, 73, 192, 1440], P('batch', None, 'lat'), may hold values from -64 to 64
- target: bfloat16 [4, 73, 192, 1440], P('batch', None, 'lat'), may hold values from -128 to 128
- legendre_basis: bfloat16 [192, 96, 720], P(None, ('batch', 'lat')), may hold values from -1 to 1
Outputs:
- spectra: float32 [2, 73, 720], replicated
- channel_loss: float32 [73], replicated
All inputs are finite; a program needn't handle non-finite values.
Results may differ from a plain program's by a relative error of at most 0.0003.
Values may be sent and summed in bfloat16 or wider, within the bound.
No kernel may reach another device: no remote copies, remote signals or barrier semaphores. Data moves between devices by JAX's collectives and lax.ppermute only.
A program may use at most 128 MiB of HBM per device.

v0:
```python
import math
import jax
import jax.numpy as jnp
from jax import lax
from jax.sharding import PartitionSpec as P


def fourier_table(lon_count, order_count):
    lon_ids = jnp.arange(lon_count, dtype=jnp.int32)
    order_ids = jnp.arange(order_count, dtype=jnp.int32)
    product_ids = lon_ids[:, None] * order_ids[None, :] % lon_count
    angles = 2.0 * math.pi / lon_count * product_ids.astype(jnp.float32)
    inv_root = 1.0 / math.sqrt(lon_count)
    return jnp.stack([jnp.cos(angles) * inv_root, -jnp.sin(angles) * inv_root], axis=1).astype(
        jnp.bfloat16
    )


def band_energy(fourier, basis_block, orders):
    coefficients = jnp.einsum(
        "fpmbcn,nml->fpmbcl", fourier, basis_block, preferred_element_type=jnp.float32
    )
    squares = jnp.sum(coefficients * coefficients, axis=1)
    weights = jnp.where(orders == 0, 1.0, 2.0).astype(jnp.float32)
    return jnp.sum(squares * weights[None, :, None, None, None], axis=(1, 2))


def body(predicted, target, legendre_basis):
    groups = lax.axis_size("batch")
    band_count = lax.axis_size("lat")
    per_dev = legendre_basis.shape[1]
    order_count = per_dev * groups * band_count
    dft_table = fourier_table(predicted.shape[3], order_count)
    band_id = lax.axis_index("lat")

    def transform(field_in):
        return jnp.einsum(
            "bcnk,kpm->pmbcn", field_in, dft_table, preferred_element_type=jnp.float32
        ).astype(jnp.bfloat16)

    fourier = jnp.stack([transform(predicted), transform(target)], axis=0)
    members = fourier.shape[3]
    channels = fourier.shape[4]
    lat_rows = fourier.shape[5]
    fourier = fourier.reshape(2, 2, groups, band_count, per_dev, members, channels, lat_rows)
    arrived = lax.all_to_all(fourier, "lat", split_axis=3, concat_axis=7, tiled=True)
    arrived = arrived.reshape(
        2, 2, groups * per_dev, arrived.shape[5], arrived.shape[6], arrived.shape[7]
    )
    basis_block = lax.all_gather(legendre_basis, "batch", axis=1, tiled=True)
    taken = basis_block.shape[1]
    gathered_ids = jnp.arange(taken, dtype=jnp.int32)
    orders = (
        gathered_ids // per_dev * band_count * per_dev + band_id * per_dev + gathered_ids % per_dev
    )
    partial_value = band_energy(arrived, basis_block, orders)
    energy = lax.psum(partial_value, "lat")
    energy = lax.psum(energy, "batch")
    spectra = energy / (predicted.shape[0] * groups * order_count)
    log_spectra = jnp.log(spectra + 1e-06)
    channel_loss = jnp.mean((log_spectra[0] - log_spectra[1]) ** 2, axis=1)
    return (spectra, channel_loss)


def solution(mesh):
    placed = (
        P("batch", None, "lat", None),
        P("batch", None, "lat", None),
        P(None, ("batch", "lat"), None),
    )
    return jax.shard_map(body, mesh=mesh, in_specs=placed, out_specs=(P(), P()), check_vma=False)
```

profile of v0, /device:TPU:0, one launch (start us, length us, event | category | flops | bytes accessed | tf_op | source)
XLA Modules:
  0.0 212.2 jit_solution(11625327290755649896)
XLA Ops:
  7.2 0.0 all-gather.2.cloned.1.call-start
  7.2 0.7 all-gather.2.cloned.1.call-update
  7.9 2.6 %multiply_convert_fusion = (bf16[1440,1,96]{0,2,1:T(8,128)(2,1)S(1)}, bf16[1440,1,96]{0,2,1:T(8,128)(2,1)S(1)}) fusion(), kind=kLoop, calls=%fused_computation.17 | loop fusion | flops 1935360 | bytes 552960 | tf_op jit(solution)/shard_map/convert.1
  10.5 0.0 copy-start
  10.5 0.0 copy-start.1
  10.5 0.7 copy-done
  11.2 0.1 copy-done.1
  11.3 4.8 %fusion.8 = bf16[2,96,73,24]{1,2,3,0:T(8,128)(2,1)S(1)} fusion(bf16[73,24,1440]{2,1,0:T(8,128)(2,1)} %bitcast.33, bf16[1440,1,96]{0,2,1:T(8,128)(2,1)S(1)} %get-tuple-element.4, bf16[1440,1,96]{0,2,1:T(8,128)(2,1)S(1)} %get-tuple-element.5), kind=kOutput, calls=%fused_computation.11 | convolution fusion | flops 970228224 | bytes 6271488 | tf_op jit(solution)/shard_map/bcnk,kpm->pmbcn/dot_general | solution.py:37
  16.1 0.9 copy.29
  17.0 5.5 %fusion.11 = bf16[2,96,73,24]{1,2,3,0:T(8,128)(2,1)S(1)} fusion(bf16[73,24,1440]{2,1,0:T(8,128)(2,1)} %bitcast.34, bf16[1440,1,96]{0,2,1:T(8,128)(2,1)} %copy-done, bf16[1440,1,96]{0,2,1:T(8,128)(2,1)} %copy-done.1), kind=kOutput, calls=%fused_computation.12 | convolution fusion | flops 970228224 | bytes 6271488 | tf_op jit(solution)/shard_map/bcnk,kpm->pmbcn/dot_general | solution.py:37
  22.5 0.9 copy.31
  23.3 0.5 pad_maximum_fusion
  23.9 2.0 copy.32
  25.9 7.5 %all-to-all-start = ((bf16[2,2,4,8,3,1,73,24]{6,7,4,2,1,5,0,3:T(8,128)(2,1)}), bf16[2,2,4,8,3,1,73,24]{6,7,4,2,1,5,0,3:T(8,128)(2,1)S(1)}, u32[]{:S(2)}, u32[]{:S(2)}) async-start(bf16[2,2,4,8,3,1,73,24]{6,7,4,2,1,5,0,3:T(8,128)(2,1)} %copy.32), calls=%async_computation | async-start | bytes 4718592 | tf_op jit(solution)/shard_map/all_to_all | solution.py:46
  33.5 0.0 all-reduce.3.cloned.1.call-start
  33.5 53.6 %all-to-all-done = bf16[2,2,4,8,3,1,73,24]{6,7,4,2,1,5,0,3:T(8,128)(2,1)S(1)} async-done(((bf16[2,2,4,8,3,1,73,24]{6,7,4,2,1,5,0,3:T(8,128)(2,1)}), bf16[2,2,4,8,3,1,73,24]{6,7,4,2,1,5,0,3:T(8,128)(2,1)S(1)}, u32[]{:S(2)}, u32[]{:S(2)}) %all-to-all-start) | async-done | bytes 1345568 | tf_op jit(solution)/shard_map/all_to_all | solution.py:46
  87.1 2.1 copy.33
  89.2 0.0 all-gather.2.cloned.1.call-done
  89.2 5.1 %multiply_reduce_fusion = f32[12,2,73,720]{3,2,1,0:T(8,128)S(1)} fusion(bf16[192,12,720]{2,0,1:T(8,128)(2,1)} %all-gather.2.cloned.1.call-done, bf16[2,2,12,73,192]{3,4,2,1,0:T(8,128)(2,1)} %bitcast.30), kind=kOutput, calls=%fused_computation | convolution fusion | flops 972570240 | bytes 9709056 | tf_op jit(solution)/shard_map/fpmbcn,nml->fpmbcl/dot_general | solution.py:20
  94.3 0.6 multiply_reduce_fusion.1
  94.9 1.1 copy.40
  96.0 0.0 all-reduce.3.cloned.1.call-update
  96.1 0.0 all-reduce.5.cloned.1.call-start
  96.1 71.4 %all-reduce.3.cloned.1.call-done = f32[2,73,720]{2,0,1:T(2,128)} async-done(((f32[2,73,720]{2,0,1:T(2,128)}), f32[2,73,720]{2,0,1:T(2,128)}) %all-reduce.3.cloned.1.call-update) | async-done | bytes 420496 | tf_op jit(solution)/shard_map/psum | solution.py:57
  167.5 0.0 all-reduce.5.cloned.1.call-update
  167.6 34.7 %all-reduce.5.cloned.1.call-done = f32[2,73,720]{2,0,1:T(2,128)} async-done(((f32[2,73,720]{2,0,1:T(2,128)}), f32[2,73,720]{2,0,1:T(2,128)}) %all-reduce.5.cloned.1.call-update) | async-done | bytes 420496 | tf_op jit(solution)/shard_map/psum | solution.py:58
  202.2 2.2 %add_log_fusion = (f32[2,73,720]{2,0,1:T(2,128)S(1)}, f32[2,73,720]{2,0,1:T(2,128)}) fusion(f32[2,73,720]{2,0,1:T(2,128)} %all-reduce.5.cloned.1.call-done), kind=kLoop, calls=%fused_computation.23 | loop fusion | flops 210240 | bytes 1261440 | tf_op jit(solution)/shard_map/log | solution.py:60
  204.5 0.6 fusion.20
  205.1 0.5 broadcast_multiply_fusion.1
  (1 shorter events, 0.0 us)
Async XLA Ops:
  7.2 82.1 %all-gather.2.cloned.1.call-start = ((), (), s32[]{:S(2)}) async-start(), calls=%async_computation.1 | async-start | bytes 4423680 | tf_op jit(solution)/shard_map/all_gather | solution.py:50
  10.5 0.7 copy-start
  10.5 0.8 copy-start.1
  25.9 61.2 %all-to-all-start = ((bf16[2,2,4,8,3,1,73,24]{6,7,4,2,1,5,0,3:T(8,128)(2,1)}), bf16[2,2,4,8,3,1,73,24]{6,7,4,2,1,5,0,3:T(8,128)(2,1)S(1)}, u32[]{:S(2)}, u32[]{:S(2)}) async-start(bf16[2,2,4,8,3,1,73,24]{6,7,4,2,1,5,0,3:T(8,128)(2,1)} %copy.32), calls=%async_computation | async-start | bytes 4718592 | tf_op jit(solution)/shard_map/all_to_all | solution.py:46
  33.5 134.1 %all-reduce.3.cloned.1.call-start = ((), (), s32[]{:S(2)}) async-start(), calls=%async_computation.2 | async-start | bytes 897024 | tf_op jit(solution)/shard_map/psum | solution.py:57
  96.1 106.2 %all-reduce.5.cloned.1.call-start = ((), (), s32[]{:S(2)}) async-start(), calls=%async_computation.3 | async-start | bytes 897024 | tf_op jit(solution)/shard_map/psum | solution.py:58
Sparse Core Ops, SparseCore 0:
  9.5 33.4 all-gather.1
  96.2 71.2 all-reduce.2
  169.9 32.2 all-reduce.4
where the time goes:
time: 212 us
  waiting for transfers between devices  160 us (75%)
  matrix products  15.4 us (7%)
  between operations  13.8 us (7%)
  local copies, waits for them, and re-layouts  7.77 us (4%)
  starting transfers between devices  7.66 us (4%)
  other arithmetic  7.07 us (3%)
    psum x1, waiting for transfers between devices, body(): energy = lax.psum(partial_value, 'lat')  71.4 us
    all_to_all x1, waiting for transfers between devices, body(): lax.all_to_all(fourier, 'lat', split_axis=3, concat_axis=7, tiled=True)  53.6 us
    psum x1, waiting for transfers between devices, body(): energy = lax.psum(energy, 'batch')  34.7 us
    dot_general x2, matrix products, transform(): jnp.einsum('bcnk,kpm->pmbcn', field_in, dft_table, preferred_element_type...  10.3 us
    all_to_all x1, starting transfers between devices, body(): lax.all_to_all(fourier, 'lat', split_axis=3, concat_axis=7, tiled=True)  7.55 us
    dot_general x1, matrix products, band_energy(): jnp.einsum('fpmbcn,nml->fpmbcl', fourier, basis_block, preferred_element_...  5.1 us
  transfers between devices with their start and end apart: 4, of which 3 were waited for; matrix products, arithmetic and copies ran while one was open for 9% of the time, Pallas kernels for 0%

commit v1 on v0

--- a/solution.py
+++ b/solution.py
@@ -54,7 +54,7 @@
         gathered_ids // per_dev * band_count * per_dev + band_id * per_dev + gathered_ids % per_dev
     )
     partial_value = band_energy(arrived, basis_block, orders)
-    energy = lax.psum(partial_value, "lat")
+    energy = jnp.sum(lax.all_gather(partial_value, "lat"), axis=0)
     energy = lax.psum(energy, "batch")
     spectra = energy / (predicted.shape[0] * groups * order_count)
     log_spectra = jnp.log(spectra + 1e-06)

time: 212 us -> 209 us (0.986)
  waiting for transfers between devices: 160 us -> 155 us
  other arithmetic: 7.07 us -> 9.42 us
    psum x1 -> x0, waiting for transfers between devices: 71.4 us -> none  [body(): energy = lax.psum(partial_value, 'lat')]
    all_gather x0 -> x1, waiting for transfers between devices: none -> 68.7 us  [body(): energy = jnp.sum(lax.all_gather(partial_value, 'lat'), axis=0)]
    reduce_sum x0 -> x1, other arithmetic: none -> 3.19 us  [body(): energy = jnp.sum(lax.all_gather(partial_value, 'lat'), axis=0)]
    psum x1, waiting for transfers between devices: 34.7 us -> 32.1 us  [body(): energy = lax.psum(energy, 'batch')]
where the time goes in v1:
time: 209 us
  waiting for transfers between devices  155 us (74%)
  matrix products  15.4 us (7%)
  between operations  13.8 us (7%)
  other arithmetic  9.42 us (5%)
  local copies, waits for them, and re-layouts  7.77 us (4%)
  starting transfers between devices  7.66 us (4%)
    all_gather x1, waiting for transfers between devices, body(): energy = jnp.sum(lax.all_gather(partial_value, 'lat'), axis=0)  68.7 us
    all_to_all x1, waiting for transfers between devices, body(): lax.all_to_all(fourier, 'lat', split_axis=3, concat_axis=7, tiled=True)  53.6 us
    psum x1, waiting for transfers between devices, body(): energy = lax.psum(energy, 'batch')  32.1 us
    dot_general x2, matrix products, transform(): jnp.einsum('bcnk,kpm->pmbcn', field_in, dft_table, preferred_element_type...  10.3 us
    all_to_all x1, starting transfers between devices, body(): lax.all_to_all(fourier, 'lat', split_axis=3, concat_axis=7, tiled=True)  7.55 us
    dot_general x1, matrix products, band_energy(): jnp.einsum('fpmbcn,nml->fpmbcl', fourier, basis_block, preferred_element_...  5.1 us
  transfers between devices with their start and end apart: 4, of which 3 were waited for; matrix products, arithmetic and copies ran while one was open for 9% of the time, Pallas kernels for 0%

profile of v1, /device:TPU:0, one launch (start us, length us, event | category | flops | bytes accessed | tf_op | source)
XLA Modules:
  0.0 209.2 jit_solution(16903829719918162033)
XLA Ops:
  7.2 0.0 all-gather.4.cloned.1.call-start
  7.2 0.7 all-gather.4.cloned.1.call-update
  7.9 2.6 %multiply_convert_fusion = (bf16[1440,1,96]{0,2,1:T(8,128)(2,1)S(1)}, bf16[1440,1,96]{0,2,1:T(8,128)(2,1)S(1)}) fusion(), kind=kLoop, calls=%fused_computation.17 | loop fusion | flops 1935360 | bytes 552960 | tf_op jit(solution)/shard_map/convert.1
  10.5 0.0 copy-start
  10.5 0.0 copy-start.1
  10.5 0.7 copy-done
  11.2 0.1 copy-done.1
  11.3 4.8 %fusion.8 = bf16[2,96,73,24]{1,2,3,0:T(8,128)(2,1)S(1)} fusion(bf16[73,24,1440]{2,1,0:T(8,128)(2,1)} %bitcast.35, bf16[1440,1,96]{0,2,1:T(8,128)(2,1)S(1)} %get-tuple-element.10, bf16[1440,1,96]{0,2,1:T(8,128)(2,1)S(1)} %get-tuple-element.11), kind=kOutput, calls=%fused_computation.11 | convolution fusion | flops 970228224 | bytes 6271488 | tf_op jit(solution)/shard_map/bcnk,kpm->pmbcn/dot_general | solution.py:37
  16.1 0.9 copy.39
  17.0 5.5 %fusion.11 = bf16[2,96,73,24]{1,2,3,0:T(8,128)(2,1)S(1)} fusion(bf16[73,24,1440]{2,1,0:T(8,128)(2,1)} %bitcast.36, bf16[1440,1,96]{0,2,1:T(8,128)(2,1)} %copy-done, bf16[1440,1,96]{0,2,1:T(8,128)(2,1)} %copy-done.1), kind=kOutput, calls=%fused_computation.12 | convolution fusion | flops 970228224 | bytes 6271488 | tf_op jit(solution)/shard_map/bcnk,kpm->pmbcn/dot_general | solution.py:37
  22.5 0.9 copy.41
  23.3 0.5 pad_maximum_fusion
  23.9 2.0 copy.42
  25.9 7.5 %all-to-all-start = ((bf16[2,2,4,8,3,1,73,24]{6,7,4,2,1,5,0,3:T(8,128)(2,1)}), bf16[2,2,4,8,3,1,73,24]{6,7,4,2,1,5,0,3:T(8,128)(2,1)S(1)}, u32[]{:S(2)}, u32[]{:S(2)}) async-start(bf16[2,2,4,8,3,1,73,24]{6,7,4,2,1,5,0,3:T(8,128)(2,1)} %copy.42), calls=%async_computation | async-start | bytes 4718592 | tf_op jit(solution)/shard_map/all_to_all | solution.py:46
  33.5 0.0 all-gather.6.cloned.1.call-start
  33.5 53.6 %all-to-all-done = bf16[2,2,4,8,3,1,73,24]{6,7,4,2,1,5,0,3:T(8,128)(2,1)S(1)} async-done(((bf16[2,2,4,8,3,1,73,24]{6,7,4,2,1,5,0,3:T(8,128)(2,1)}), bf16[2,2,4,8,3,1,73,24]{6,7,4,2,1,5,0,3:T(8,128)(2,1)S(1)}, u32[]{:S(2)}, u32[]{:S(2)}) %all-to-all-start) | async-done | bytes 1345568 | tf_op jit(solution)/shard_map/all_to_all | solution.py:46
  87.1 2.1 %copy.43 = bf16[2,2,4,1,3,1,73,8,24]{6,8,7,4,2,1,0,5,3:T(8,128)(2,1)} copy(bf16[2,2,4,1,3,1,73,8,24]{6,8,4,2,1,0,7,5,3:T(8,128)(2,1)S(1)} %bitcast.30) | data formatting | bytes 2691072 | tf_op jit(solution)/shard_map/all_to_all | solution.py:46
  89.2 0.0 all-gather.4.cloned.1.call-done
  89.2 5.1 %multiply_reduce_fusion = f32[12,2,73,720]{3,2,1,0:T(8,128)S(1)} fusion(bf16[192,12,720]{2,0,1:T(8,128)(2,1)} %all-gather.4.cloned.1.call-done, bf16[2,2,12,73,192]{3,4,2,1,0:T(8,128)(2,1)} %bitcast.31), kind=kOutput, calls=%fused_computation | convolution fusion | flops 972570240 | bytes 9709056 | tf_op jit(solution)/shard_map/fpmbcn,nml->fpmbcl/dot_general | solution.py:20
  94.3 1.3 multiply_reduce_fusion.1
  95.7 0.0 all-gather.6.cloned.1.call-update
  95.7 0.0 all-reduce.2.cloned.1.call-start
  95.8 68.7 %all-gather.6.cloned.1.call-done = f32[16,73,720]{2,1,0:T(8,128)} async-done(((f32[2,73,720]{2,1,0:T(8,128)}), f32[16,73,720]{2,1,0:T(8,128)}) %all-gather.6.cloned.1.call-update) | async-done | bytes 3363856 | tf_op jit(solution)/shard_map/all_gather | solution.py:57
  164.4 3.2 %reduce_sum.38 = f32[2,73,720]{2,1,0:T(8,128)} reduce(f32[8,2,73,720]{3,2,1,0:T(8,128)} %bitcast.34, f32[]{:T(128)} %constant.47.clone.1), dimensions={0}, to_apply=%region_2.3 | reduce | flops 735840 | bytes 3784324 | tf_op jit(solution)/shard_map/reduce_sum | solution.py:57
  167.6 0.0 all-reduce.2.cloned.1.call-update
  167.6 32.1 %all-reduce.2.cloned.1.call-done = f32[2,73,720]{2,1,0:T(8,128)} async-done(((f32[2,73,720]{2,1,0:T(8,128)}), f32[2,73,720]{2,1,0:T(8,128)}) %all-reduce.2.cloned.1.call-update) | async-done | bytes 420496 | tf_op jit(solution)/shard_map/psum | solution.py:58
  199.7 1.1 add_log_fusion
  200.9 1.1 copy.47
  202.0 0.1 fusion.20
  202.1 0.5 broadcast_multiply_fusion.1
  (1 shorter events, 0.0 us)
Async XLA Ops:
  7.2 82.1 %all-gather.4.cloned.1.call-start = ((), (), s32[]{:S(2)}) async-start(), calls=%async_computation.1 | async-start | bytes 4423680 | tf_op jit(solution)/shard_map/all_gather | solution.py:50
  10.5 0.7 copy-start
  10.5 0.8 copy-start.1
  25.9 61.2 %all-to-all-start = ((bf16[2,2,4,8,3,1,73,24]{6,7,4,2,1,5,0,3:T(8,128)(2,1)}), bf16[2,2,4,8,3,1,73,24]{6,7,4,2,1,5,0,3:T(8,128)(2,1)S(1)}, u32[]{:S(2)}, u32[]{:S(2)}) async-start(bf16[2,2,4,8,3,1,73,24]{6,7,4,2,1,5,0,3:T(8,128)(2,1)} %copy.42), calls=%async_computation | async-start | bytes 4718592 | tf_op jit(solution)/shard_map/all_to_all | solution.py:46
  33.5 131.0 %all-gather.6.cloned.1.call-start = ((), (), s32[]{:S(2)}) async-start(), calls=%async_computation.3 | async-start | bytes 4423680 | tf_op jit(solution)/shard_map/all_gather | solution.py:57
  95.7 104.0 %all-reduce.2.cloned.1.call-start = ((), (), s32[]{:S(2)}) async-start(), calls=%async_computation.2 | async-start | bytes 983040 | tf_op jit(solution)/shard_map/psum | solution.py:58
Sparse Core Ops, SparseCore 0:
  9.5 33.4 all-gather.3
  95.8 68.5 all-gather.5
  167.8 31.9 all-reduce.1
